TPU v7x, 32 devices: a whole 2x2x4 slice. The times are simulated.
32 devices in a mesh: seq: 8 (over z, x), tensor: 4 (over y, core).
Axes of the slice: x: 2, y: 2, z: 4, core: 2. Of those that a mesh axis runs over, the one named last changes fastest.
Arguments:
- tokens: bfloat16 [4096, 2048], P('seq', 'tensor'), may hold values from -12 to 12
- attn_gain: float32 [2048], replicated, may hold values from 0.1 to 1.9
- w_query: bfloat16 [2048, 2048], P('seq', 'tensor'), as said below
- w_key: bfloat16 [2048, 512], P('seq', 'tensor'), as said below
- w_value: bfloat16 [2048, 512], P('seq', 'tensor'), may hold values from -0.125 to 0.125
- w_out: bfloat16 [2048, 2048], P('tensor', 'seq'), may hold values from -0.125 to 0.125
- mlp_gain: float32 [2048], replicated, may hold values from 0.1 to 1.9
- w_gate: bfloat16 [2048, 5632], P('seq', 'tensor'), may hold values from -0.125 to 0.125
- w_up: bfloat16 [2048, 5632], P('seq', 'tensor'), may hold values from -0.125 to 0.125
- w_down: bfloat16 [5632, 2048], P('tensor', 'seq'), may hold values from -0.078125 to 0.078125
Outputs:
- layer_out: bfloat16 [4096, 2048], P('seq', 'tensor')
Inputs may be any that keep to these rules, and one draw needn't show every extreme that they name: `w_query`: entries are of order 2048 to the power -1/2. `w_key`: entries are of order 2048 to the power -1/2.
All inputs are finite; a program needn't handle non-finite values.
Results may differ from a plain program's by a relative error of at most 0.013.
Values may be sent and summed in bfloat16 or wider, within the bound.
A program may use at most 128 MiB of HBM per device.

v0:
```python
import jax
import jax.numpy as jnp
from jax import lax
from jax.sharding import PartitionSpec as P

HEAD_DIM = 128
WINDOW = 1024


def passed_along(block, axis, distance):
    devices = range(lax.axis_size(axis))
    route = [(i - distance, i) for i in devices if i - distance in devices]
    return lax.ppermute(block, axis, route)


def scaled_rows(values, gain):
    values = values.astype(jnp.float32)
    mean_square = jnp.mean(values * values, axis=1, keepdims=True)
    return (values * lax.rsqrt(mean_square + 1e-06) * gain).astype(jnp.bfloat16)


def product(left, right):
    return jnp.dot(left, right, preferred_element_type=jnp.float32)


def window_attention(queries, context_keys, context_values, reach, position):
    rows = queries.shape[0]
    local_kv = context_keys.shape[1] // HEAD_DIM
    group = queries.shape[1] // (local_kv * HEAD_DIM)
    block = min(512, rows)
    span = WINDOW + block
    scale = HEAD_DIM ** (-0.5)
    start = reach * rows - WINDOW
    query_block = queries.reshape(block, local_kv, group, HEAD_DIM)
    key_block = context_keys.reshape(span, local_kv, HEAD_DIM)
    value_block = context_values.reshape(span, local_kv, HEAD_DIM)
    scores = (
        jnp.einsum("qkgd,ckd->kgqc", query_block, key_block, preferred_element_type=jnp.float32)
        * scale
    )
    query_pos = lax.broadcasted_iota(jnp.int32, (block, span), 0)
    key_pos = lax.broadcasted_iota(jnp.int32, (block, span), 1)
    distance = query_pos + WINDOW - key_pos
    first_key = (position - reach) * rows + start
    allowed = (distance >= 0) & (distance < WINDOW) & (key_pos + first_key >= 0)
    scores = jnp.where(allowed[None, None], scores, -1e30)
    highest = jnp.max(scores, axis=3, keepdims=True)
    raised = jnp.exp(scores - highest)
    weights = (raised / jnp.sum(raised, axis=3, keepdims=True)).astype(jnp.bfloat16)
    mixed = jnp.einsum("kgqc,ckd->qkgd", weights, value_block, preferred_element_type=jnp.float32)
    outputs = mixed.astype(jnp.bfloat16).reshape(block, local_kv * group * HEAD_DIM)
    return outputs


def per_device(tokens, attn_gain, w_query, w_key, w_value, w_out, mlp_gain, w_gate, w_up, w_down):
    rows = tokens.shape[0]
    whole = lax.all_gather(tokens, "tensor", axis=1, tiled=True)
    normed = scaled_rows(whole, attn_gain)
    query_full = lax.all_gather(w_query, "seq", axis=0, tiled=True)
    key_full, value_full = (
        lax.all_gather(w_key, "seq", axis=0, tiled=True),
        lax.all_gather(w_value, "seq", axis=0, tiled=True),
    )
    queries = product(normed, query_full).astype(jnp.bfloat16)
    keys = product(normed, key_full).astype(jnp.bfloat16)
    values = product(normed, value_full).astype(jnp.bfloat16)
    reach = -(-WINDOW // rows)
    earlier = []
    for step in range(reach):
        earlier.append(passed_along((keys, values), "seq", step + 1))
    context_keys = jnp.concatenate(
        [earlier[reach - 1 - step][0] for step in range(reach)] + [keys], axis=0
    )
    context_values = jnp.concatenate(
        [earlier[reach - 1 - step][1] for step in range(reach)] + [values], axis=0
    )
    position = lax.axis_index("seq")
    attended = window_attention(queries, context_keys, context_values, reach, position)
    out_full = lax.all_gather(w_out, "seq", axis=1, tiled=True)
    head_terms = product(attended, out_full)
    share = tokens.shape[1]
    attn_whole = lax.psum(head_terms.astype(jnp.bfloat16), "tensor").astype(jnp.float32)
    stream_whole = (whole.astype(jnp.float32) + attn_whole).astype(jnp.bfloat16)
    stream_share = lax.dynamic_slice_in_dim(
        stream_whole, lax.axis_index("tensor") * share, share, 1
    )
    stream_normed = scaled_rows(stream_whole, mlp_gain)
    gate_full = lax.all_gather(w_gate, "seq", axis=0, tiled=True)
    up_full = lax.all_gather(w_up, "seq", axis=0, tiled=True)
    gate = product(stream_normed, gate_full)
    upward = product(stream_normed, up_full)
    hidden = (jax.nn.silu(gate) * upward).astype(jnp.bfloat16)
    down_full = lax.all_gather(w_down, "seq", axis=1, tiled=True)
    unit_terms = product(hidden, down_full)
    mlp_share = lax.psum_scatter(
        unit_terms.astype(jnp.bfloat16), "tensor", scatter_dimension=1, tiled=True
    ).astype(jnp.float32)
    return (stream_share.astype(jnp.float32) + mlp_share).astype(jnp.bfloat16)


def solution(mesh):
    in_specs = (
        P("seq", "tensor"),
        P(),
        P("seq", "tensor"),
        P("seq", "tensor"),
        P("seq", "tensor"),
        P("tensor", "seq"),
        P(),
        P("seq", "tensor"),
        P("seq", "tensor"),
        P("tensor", "seq"),
    )
    out_specs = P("seq", "tensor")
    return jax.shard_map(
        per_device, mesh=mesh, in_specs=in_specs, out_specs=out_specs, check_vma=False
    )
```

profile of v0, /device:TPU:0, one launch (start us, length us, event | category | flops | bytes accessed | tf_op | source)
XLA Modules:
  0.0 529.0 jit_solution(15447656682437301794)
XLA Ops:
  6.5 0.7 all-gather.7.cloned.1.call-update
  7.3 0.0 all-gather.9.cloned.1.call-start
  7.3 0.7 all-gather.9.cloned.1.call-update
  8.0 0.0 all-gather.11.cloned.1.call-start
  8.1 0.7 all-gather.11.cloned.1.call-update
  8.7 0.0 all-reduce.2.cloned.1.call-start
  8.8 33.4 %all_gather.26 = bf16[2048,128]{1,0:T(8,128)(2,1)S(1)} all-gather(bf16[256,128]{1,0:T(8,128)(2,1)} %param.13), channel_id=1, replica_groups=mesh['seq'=8,'tensor'=4] {'seq'}, dimensions={0}, use_global_device_ids=true | all-gather | bytes 589824 | tf_op jit(solution)/shard_map/all_gather | solution.py:61
  42.2 35.2 %all_gather.25 = bf16[2048,128]{1,0:T(8,128)(2,1)} all-gather(bf16[256,128]{1,0:T(8,128)(2,1)} %param.14), channel_id=1, replica_groups=mesh['seq'=8,'tensor'=4] {'seq'}, dimensions={0}, use_global_device_ids=true | all-gather | bytes 589824 | tf_op jit(solution)/shard_map/all_gather | solution.py:62
  77.3 1.3 fusion.14
  78.6 0.0 all-gather.7.cloned.1.call-done
  78.7 2.2 fusion.7
  80.9 2.4 convolution_convert_fusion.3
  83.3 1.3 collective-permute-start.2
  84.6 4.3 collective-permute-start.3
  88.9 0.8 convolution_convert_fusion.4
  89.6 2.7 collective-permute-start
  92.4 2.7 collective-permute-start.1
  95.1 0.0 all-gather.9.cloned.1.call-done
  95.1 3.0 convolution_convert_fusion.2
  98.1 0.0 collective-permute-done.2
  98.1 0.0 collective-permute-done.3
  98.1 3.3 fusion.1
  101.4 2.8 fusion
  104.2 0.0 collective-permute-done
  104.2 0.0 collective-permute-done.1
  104.2 4.8 fusion.16
  109.0 33.7 %all-gather.11.cloned.1.call-done = bf16[512,2048]{1,0:T(8,128)(2,1)} async-done(((bf16[512,256]{1,0:T(8,128)(2,1)}), bf16[512,2048]{1,0:T(8,128)(2,1)}) %all-gather.11.cloned.1.call-update) | async-done | bytes 2097168 | tf_op jit(solution)/shard_map/all_gather | solution.py:79
  142.7 4.4 convolution_convert_fusion
  147.1 0.0 all-reduce.2.cloned.1.call-update
  147.1 0.0 copy-start.4
  147.1 0.0 all-gather.13.cloned.1.call-start
  147.2 0.5 all-gather.13.cloned.1.call-update
  147.7 0.0 all-gather.15.cloned.1.call-start
  147.8 0.5 all-gather.15.cloned.1.call-update
  148.3 0.0 all-gather.17.cloned.1.call-start
  148.4 0.7 all-gather.17.cloned.1.call-update
  149.1 0.3 reduce-scatter.2.cloned.1.call-start
  149.3 47.5 %all-reduce.2.cloned.1.call-done = bf16[512,2048]{1,0:T(8,128)(2,1)} async-done(((bf16[512,2048]{1,0:T(8,128)(2,1)}), bf16[512,2048]{1,0:T(8,128)(2,1)}) %all-reduce.2.cloned.1.call-update) | async-done | bytes 2097168 | tf_op jit(solution)/shard_map/psum | solution.py:82
  196.9 3.9 fusion.4
  200.8 90.5 %all-gather.13.cloned.1.call-done = bf16[2048,1408]{1,0:T(8,128)(2,1)} async-done(((bf16[256,1408]{1,0:T(8,128)(2,1)}), bf16[2048,1408]{1,0:T(8,128)(2,1)}) %all-gather.13.cloned.1.call-update) | async-done | bytes 5767184 | tf_op jit(solution)/shard_map/all_gather | solution.py:88
  291.3 8.4 %fusion.21 = f32[512,1408]{1,0:T(8,128)} fusion(bf16[2048,1408]{1,0:T(8,128)(2,1)} %all-gather.13.cloned.1.call-done, bf16[512,2048]{1,0:T(8,128)(2,1)} %get-tuple-element.6, f32[2048]{0:T(1024)S(1)} %copy-done.4, f32[512]{0:T(512)S(1)} %add_rsqrt_fusion), kind=kOutput, calls=%fused_computation.33 | convolution fusion | flops 2956984320 | bytes 10758144 | tf_op jit(solution)/shard_map/dot_general | solution.py:23
  299.7 84.1 %all-gather.15.cloned.1.call-done = bf16[2048,1408]{1,0:T(8,128)(2,1)} async-done(((bf16[256,1408]{1,0:T(8,128)(2,1)}), bf16[2048,1408]{1,0:T(8,128)(2,1)}) %all-gather.15.cloned.1.call-update) | async-done | bytes 5767184 | tf_op jit(solution)/shard_map/all_gather | solution.py:89
  383.9 93.4 %all-gather.17.cloned.1.call-done = bf16[1408,2048]{1,0:T(8,128)(2,1)} async-done(((bf16[1408,256]{1,0:T(8,128)(2,1)}), bf16[1408,2048]{1,0:T(8,128)(2,1)}) %all-gather.17.cloned.1.call-update) | async-done | bytes 5767184 | tf_op jit(solution)/shard_map/all_gather | solution.py:93
  477.2 0.0 copy-done.1
  477.2 13.4 %convolution_convert_fusion.1 = bf16[512,2048]{1,0:T(8,128)(2,1)} fusion(bf16[1408,2048]{1,0:T(8,128)(2,1)} %all-gather.17.cloned.1.call-done, bf16[2048,1408]{1,0:T(8,128)(2,1)} %all-gather.15.cloned.1.call-done, f32[512,1408]{1,0:T(8,128)} %fusion.21, bf16[512,2048]{1,0:T(8,128)(2,1)S(1)} %copy-done.1, f32[2048]{0:T(1024)S(1)} %copy-done.4, ...), kind=kOutput, calls=%fused_computation.27 | convolution fusion | flops 5915148288 | bytes 18622464 | tf_op jit(solution)/shard_map/dot_general | solution.py:23
  490.7 0.0 reduce-scatter.2.cloned.1.call-update
  490.7 29.5 %reduce-scatter.2.cloned.1.call-done = bf16[512,512]{1,0:T(8,128)(2,1)} async-done(((bf16[512,2048]{1,0:T(8,128)(2,1)}), bf16[512,512]{1,0:T(8,128)(2,1)}) %reduce-scatter.2.cloned.1.call-update) | async-done | bytes 524304 | tf_op jit(solution)/shard_map/reduce_scatter | solution.py:95
  520.2 2.0 add_convert_fusion
  (13 shorter events, 0.0 us)
Async XLA Ops:
  6.5 74.4 %copy-start.3 = (f32[2048]{0:T(1024)S(1)}, f32[2048]{0:T(1024)}, u32[]{:S(2)}) copy-start(f32[2048]{0:T(1024)} %param.11) | copy-start | bytes 24580
  6.5 72.1 %all-gather.7.cloned.1.call-start = ((), (), s32[]{:S(2)}) async-start(), calls=%async_computation.1 | async-start | bytes 2621440 | tf_op jit(solution)/shard_map/all_gather | solution.py:57
  7.3 87.8 %all-gather.9.cloned.1.call-start = ((), (), s32[]{:S(2)}) async-start(), calls=%async_computation.2 | async-start | bytes 2359296 | tf_op jit(solution)/shard_map/all_gather | solution.py:59
  8.0 134.7 %all-gather.11.cloned.1.call-start = ((), (), s32[]{:S(2)}) async-start(), calls=%async_computation.3 | async-start | bytes 2359296 | tf_op jit(solution)/shard_map/all_gather | solution.py:79
  8.7 188.1 %all-reduce.2.cloned.1.call-start = ((), (), s32[]{:S(2)}) async-start(), calls=%async_computation.4 | async-start | bytes 4194304 | tf_op jit(solution)/shard_map/psum | solution.py:82
  78.6 10.2 %copy-start = (bf16[512,2048]{1,0:T(8,128)(2,1)S(1)}, bf16[512,2048]{1,0:T(8,128)(2,1)}, u32[]{:S(2)}) copy-start(bf16[512,2048]{1,0:T(8,128)(2,1)} %all-gather.7.cloned.1.call-done) | copy-start | bytes 6291460
  78.7 10.2 %copy-start.2 = (bf16[2048,128]{1,0:T(8,128)(2,1)S(1)}, bf16[2048,128]{1,0:T(8,128)(2,1)}, u32[]{:S(2)}) copy-start(bf16[2048,128]{1,0:T(8,128)(2,1)} %all_gather.25) | copy-start | bytes 1572868
  83.3 14.8 %collective-permute-start.2 = (bf16[512,128]{1,0:T(8,128)(2,1)S(1)}, bf16[512,128]{1,0:T(8,128)(2,1)S(1)}, u32[]{:S(2)}, u32[]{:S(2)}) collective-permute-start(bf16[512,128]{1,0:T(8,128)(2,1)S(1)} %convolution_convert_fusion.3), channel_id=1, source_target_pairs={{0,8},{4,12},{8,16},{12,20},{16,24},{20,28},{1,9},{5,13},{9,17},{1... | collective-permute-start | bytes 393224 | tf_op jit(solution)/shard_map/ppermute | solution.py:13
  84.6 13.5 %collective-permute-start.3 = (bf16[512,128]{1,0:T(8,128)(2,1)S(1)}, bf16[512,128]{1,0:T(8,128)(2,1)}, u32[]{:S(2)}, u32[]{:S(2)}) collective-permute-start(bf16[512,128]{1,0:T(8,128)(2,1)S(1)} %convolution_convert_fusion.3), channel_id=1, source_target_pairs={{0,4},{4,8},{8,12},{12,16},{16,20},{20,24},{24,28},{1,5},{5,9},{9,... | collective-permute-start | bytes 393224 | tf_op jit(solution)/shard_map/ppermute | solution.py:13
  89.6 14.5 %collective-permute-start = (bf16[512,128]{1,0:T(8,128)(2,1)S(1)}, bf16[512,128]{1,0:T(8,128)(2,1)S(1)}, u32[]{:S(2)}, u32[]{:S(2)}) collective-permute-start(bf16[512,128]{1,0:T(8,128)(2,1)S(1)} %convolution_convert_fusion.4), channel_id=1, source_target_pairs={{0,8},{4,12},{8,16},{12,20},{16,24},{20,28},{1,9},{5,13},{9,17},{1... | collective-permute-start | bytes 393224 | tf_op jit(solution)/shard_map/ppermute | solution.py:13
  92.4 11.8 %collective-permute-start.1 = (bf16[512,128]{1,0:T(8,128)(2,1)S(1)}, bf16[512,128]{1,0:T(8,128)(2,1)S(1)}, u32[]{:S(2)}, u32[]{:S(2)}) collective-permute-start(bf16[512,128]{1,0:T(8,128)(2,1)S(1)} %convolution_convert_fusion.4), channel_id=1, source_target_pairs={{0,4},{4,8},{8,12},{12,16},{16,20},{20,24},{24,28},{1,5},{5,9},{9,... | collective-permute-start | bytes 393224 | tf_op jit(solution)/shard_map/ppermute | solution.py:13
  147.1 144.2 %copy-start.4 = (f32[2048]{0:T(1024)S(1)}, f32[2048]{0:T(1024)}, u32[]{:S(2)}) copy-start(f32[2048]{0:T(1024)} %param.16) | copy-start | bytes 24580
  147.1 144.1 %all-gather.13.cloned.1.call-start = ((), (), s32[]{:S(2)}) async-start(), calls=%async_computation.5 | async-start | bytes 6488064 | tf_op jit(solution)/shard_map/all_gather | solution.py:88
  147.7 236.1 %all-gather.15.cloned.1.call-start = ((), (), s32[]{:S(2)}) async-start(), calls=%async_computation.6 | async-start | bytes 6488064 | tf_op jit(solution)/shard_map/all_gather | solution.py:89
  148.3 328.9 %all-gather.17.cloned.1.call-start = ((), (), s32[]{:S(2)}) async-start(), calls=%async_computation.7 | async-start | bytes 6488064 | tf_op jit(solution)/shard_map/all_gather | solution.py:93
  149.1 371.1 %reduce-scatter.2.cloned.1.call-start = ((), (), s32[]{:S(2)}) async-start(), calls=%async_computation.8 | async-start | bytes 2621440 | tf_op jit(solution)/shard_map/reduce_scatter | solution.py:95
  291.3 185.9 %copy-start.1 = (bf16[512,2048]{1,0:T(8,128)(2,1)S(1)}, bf16[512,2048]{1,0:T(8,128)(2,1)}, u32[]{:S(2)}) copy-start(bf16[512,2048]{1,0:T(8,128)(2,1)} %get-tuple-element.6) | copy-start | bytes 6291460
Sparse Core Ops, SparseCore 0:
  8.9 25.2 all-gather.6
  36.3 52.5 all-gather.8
  91.0 51.7 all-gather.10
  147.3 49.5 all-reduce.1
  198.9 92.3 all-gather.12
  293.3 90.4 all-gather.14
  385.9 91.2 all-gather.16
  490.8 29.3 reduce-scatter.1
where the time goes:
time: 529 us
  waiting for transfers between devices  383 us (72%)
  blocking collectives  68.5 us (13%)
  matrix products  40.5 us (8%)
  between operations  13.7 us (3%)
  other arithmetic  12.2 us (2%)
  starting transfers between devices  11.5 us (2%)
    all_gather x1, waiting for transfers between devices, per_device(): down_full = lax.all_gather(w_down, 'seq', axis=1, tiled=True)  93.4 us
    all_gather x1, waiting for transfers between devices, per_device(): gate_full = lax.all_gather(w_gate, 'seq', axis=0, tiled=True)  90.5 us
    all_gather x1, waiting for transfers between devices, per_device(): up_full = lax.all_gather(w_up, 'seq', axis=0, tiled=True)  84.1 us
    psum x1, waiting for transfers between devices, per_device(): lax.psum(head_terms.astype(jnp.bfloat16), 'tensor').astype(jnp.float32)  47.5 us
    all_gather x1, blocking collectives, per_device(): lax.all_gather(w_value, 'seq', axis=0, tiled=True)  35.2 us
    all_gather x1, waiting for transfers between devices, per_device(): out_full = lax.all_gather(w_out, 'seq', axis=1, tiled=True)  33.7 us
    all_gather x1, blocking collectives, per_device(): lax.all_gather(w_key, 'seq', axis=0, tiled=True)  33.4 us
    dot_general x6, matrix products, product(): return jnp.dot(left, right, preferred_element_type=jnp.float32)  32.3 us
  transfers between devices with their start and end apart: 12, of which 6 were waited for; matrix products, arithmetic and copies ran while one was open for 6% of the time, Pallas kernels for 0%

commit v1 on v0

--- a/solution.py
+++ b/solution.py
@@ -5,6 +5,10 @@
 
 HEAD_DIM = 128
 WINDOW = 1024
+
+
+def prepare_arrays_for(tile_in, axis_key):
+    return lax.all_gather(tile_in, axis_name=axis_key).sum(axis=0)
 
 
 def passed_along(block, axis, distance):
@@ -79,7 +83,7 @@
     out_full = lax.all_gather(w_out, "seq", axis=1, tiled=True)
     head_terms = product(attended, out_full)
     share = tokens.shape[1]
-    attn_whole = lax.psum(head_terms.astype(jnp.bfloat16), "tensor").astype(jnp.float32)
+    attn_whole = prepare_arrays_for(head_terms.astype(jnp.bfloat16), "tensor").astype(jnp.float32)
     stream_whole = (whole.astype(jnp.float32) + attn_whole).astype(jnp.bfloat16)
     stream_share = lax.dynamic_slice_in_dim(
         stream_whole, lax.axis_index("tensor") * share, share, 1

time: 529 us -> 536 us (1.013)
  other arithmetic: 12.2 us -> 19.4 us
    all_gather x0 -> x1, waiting for transfers between devices: none -> 54.4 us  [prepare_arrays_for(): return lax.all_gather(tile_in, axis_name=axis_key).sum(axis=0)]
    psum x1 -> x0, waiting for transfers between devices: 47.5 us -> none  [per_device(): lax.psum(head_terms.astype(jnp.bfloat16), 'tensor').astype(jnp.float32)]
    all_gather x1, waiting for transfers between devices: 90.5 us -> 83.3 us  [per_device(): gate_full = lax.all_gather(w_gate, 'seq', axis=0, tiled=True)]
    reduce_sum x0 -> x1, other arithmetic: none -> 7.19 us  [prepare_arrays_for(): return lax.all_gather(tile_in, axis_name=axis_key).sum(axis=0)]
  transfers between devices with their start and end apart: 12 -> 12, of which waited for: 6 -> 6; matrix products, arithmetic and copies ran while one was open for 6% -> 7% of each run, Pallas kernels for 0% -> 0%
where the time goes in v1:
time: 536 us
  waiting for transfers between devices  382 us (71%)
  blocking collectives  68.5 us (13%)
  matrix products  40.4 us (8%)
  other arithmetic  19.4 us (4%)
  between operations  13.6 us (3%)
  starting transfers between devices  11.5 us (2%)
    all_gather x1, waiting for transfers between devices, per_device(): down_full = lax.all_gather(w_down, 'seq', axis=1, tiled=True)  93.4 us
    all_gather x1, waiting for transfers between devices, per_device(): up_full = lax.all_gather(w_up, 'seq', axis=0, tiled=True)  84.1 us
    all_gather x1, waiting for transfers between devices, per_device(): gate_full = lax.all_gather(w_gate, 'seq', axis=0, tiled=True)  83.3 us
    all_gather x1, waiting for transfers between devices, prepare_arrays_for(): return lax.all_gather(tile_in, axis_name=axis_key).sum(axis=0)  54.4 us
    all_gather x1, blocking collectives, per_device(): lax.all_gather(w_value, 'seq', axis=0, tiled=True)  35.1 us
    all_gather x1, waiting for transfers between devices, per_device(): out_full = lax.all_gather(w_out, 'seq', axis=1, tiled=True)  33.7 us
    all_gather x1, blocking collectives, per_device(): lax.all_gather(w_key, 'seq', axis=0, tiled=True)  33.4 us
    dot_general x6, matrix products, product(): return jnp.dot(left, right, preferred_element_type=jnp.float32)  32.3 us
  transfers between devices with their start and end apart: 12, of which 6 were waited for; matrix products, arithmetic and copies ran while one was open for 7% of the time, Pallas kernels for 0%

profile of v1, /device:TPU:0, one launch (start us, length us, event | category | flops | bytes accessed | tf_op | source)
XLA Modules:
  0.0 535.7 jit_solution(16254875460456056541)
XLA Ops:
  6.5 0.0 all-gather.9.cloned.1.call-start
  6.5 0.7 all-gather.9.cloned.1.call-update
  7.3 0.0 all-gather.11.cloned.1.call-start
  7.3 0.7 all-gather.11.cloned.1.call-update
  8.0 0.0 all-gather.13.cloned.1.call-start
  8.1 0.7 all-gather.13.cloned.1.call-update
  8.7 0.0 all-gather.21.cloned.1.call-start
  8.8 33.4 %all_gather.32 = bf16[2048,128]{1,0:T(8,128)(2,1)S(1)} all-gather(bf16[256,128]{1,0:T(8,128)(2,1)} %param.13), channel_id=1, replica_groups=mesh['seq'=8,'tensor'=4] {'seq'}, dimensions={0}, use_global_device_ids=true | all-gather | bytes 589824 | tf_op jit(solution)/shard_map/all_gather | solution.py:65
  42.2 35.1 %all_gather.31 = bf16[2048,128]{1,0:T(8,128)(2,1)} all-gather(bf16[256,128]{1,0:T(8,128)(2,1)} %param.14), channel_id=1, replica_groups=mesh['seq'=8,'tensor'=4] {'seq'}, dimensions={0}, use_global_device_ids=true | all-gather | bytes 589824 | tf_op jit(solution)/shard_map/all_gather | solution.py:66
  77.3 1.3 fusion.14
  78.6 0.0 all-gather.9.cloned.1.call-done
  78.7 2.2 fusion.7
  80.9 2.4 convolution_convert_fusion.3
  83.3 1.3 collective-permute-start.2
  84.6 4.3 collective-permute-start.3
  88.9 0.8 convolution_convert_fusion.4
  89.6 2.7 collective-permute-start
  92.4 2.7 collective-permute-start.1
  95.1 0.0 all-gather.11.cloned.1.call-done
  95.1 3.0 convolution_convert_fusion.2
  98.1 0.0 collective-permute-done.2
  98.1 0.0 collective-permute-done.3
  98.1 3.3 fusion.1
  101.4 2.8 fusion
  104.2 0.0 collective-permute-done
  104.2 0.0 collective-permute-done.1
  104.2 4.8 fusion.16
  109.0 33.7 %all-gather.13.cloned.1.call-done = bf16[512,2048]{1,0:T(8,128)(2,1)} async-done(((bf16[512,256]{1,0:T(8,128)(2,1)}), bf16[512,2048]{1,0:T(8,128)(2,1)}) %all-gather.13.cloned.1.call-update) | async-done | bytes 2097168 | tf_op jit(solution)/shard_map/all_gather | solution.py:83
  142.8 4.4 convolution_convert_fusion
  147.1 0.0 all-gather.21.cloned.1.call-update
  147.2 0.0 all-gather.15.cloned.1.call-start
  147.2 0.5 all-gather.15.cloned.1.call-update
  147.7 0.0 all-gather.17.cloned.1.call-start
  147.8 0.5 all-gather.17.cloned.1.call-update
  148.3 0.0 all-gather.19.cloned.1.call-start
  148.4 0.7 all-gather.19.cloned.1.call-update
  149.1 0.3 reduce-scatter.2.cloned.1.call-start
  149.3 54.4 %all-gather.21.cloned.1.call-done = bf16[2048,2048]{1,0:T(8,128)(2,1)} async-done(((bf16[512,2048]{1,0:T(8,128)(2,1)}), bf16[2048,2048]{1,0:T(8,128)(2,1)}) %all-gather.21.cloned.1.call-update) | async-done | bytes 8388624 | tf_op jit(solution)/shard_map/all_gather | solution.py:11
  203.8 7.2 %reduce_sum.41 = bf16[512,2048]{1,0:T(8,128)(2,1)} reduce(bf16[4,512,2048]{2,1,0:T(8,128)(2,1)} %bitcast.44, bf16[]{:T(256)} %constant.36.clone.1), dimensions={0}, to_apply=%region_3.4 | reduce | flops 3145728 | bytes 10485762 | tf_op jit(solution)/shard_map/reduce_sum | solution.py:11
  211.0 3.9 fusion.4
  214.9 83.3 %all-gather.15.cloned.1.call-done = bf16[2048,1408]{1,0:T(8,128)(2,1)} async-done(((bf16[256,1408]{1,0:T(8,128)(2,1)}), bf16[2048,1408]{1,0:T(8,128)(2,1)}) %all-gather.15.cloned.1.call-update) | async-done | bytes 5767184 | tf_op jit(solution)/shard_map/all_gather | solution.py:92
  298.1 8.4 %fusion.21 = f32[512,1408]{1,0:T(8,128)} fusion(bf16[2048,1408]{1,0:T(8,128)(2,1)} %all-gather.15.cloned.1.call-done, bf16[512,2048]{1,0:T(8,128)(2,1)} %get-tuple-element.6, f32[2048]{0:T(1024)S(1)} %copy-done.4, f32[512]{0:T(512)S(1)} %add_rsqrt_fusion), kind=kOutput, calls=%fused_computation.33 | convolution fusion | flops 2956984320 | bytes 10758144 | tf_op jit(solution)/shard_map/dot_general | solution.py:27
  306.6 84.1 %all-gather.17.cloned.1.call-done = bf16[2048,1408]{1,0:T(8,128)(2,1)} async-done(((bf16[256,1408]{1,0:T(8,128)(2,1)}), bf16[2048,1408]{1,0:T(8,128)(2,1)}) %all-gather.17.cloned.1.call-update) | async-done | bytes 5767184 | tf_op jit(solution)/shard_map/all_gather | solution.py:93
  390.7 93.4 %all-gather.19.cloned.1.call-done = bf16[1408,2048]{1,0:T(8,128)(2,1)} async-done(((bf16[1408,256]{1,0:T(8,128)(2,1)}), bf16[1408,2048]{1,0:T(8,128)(2,1)}) %all-gather.19.cloned.1.call-update) | async-done | bytes 5767184 | tf_op jit(solution)/shard_map/all_gather | solution.py:97
  484.1 13.3 %convolution_convert_fusion.1 = bf16[512,2048]{1,0:T(8,128)(2,1)} fusion(bf16[1408,2048]{1,0:T(8,128)(2,1)} %all-gather.19.cloned.1.call-done, bf16[2048,1408]{1,0:T(8,128)(2,1)} %all-gather.17.cloned.1.call-done, f32[512,1408]{1,0:T(8,128)} %fusion.21, bf16[512,2048]{1,0:T(8,128)(2,1)S(1)} %copy-done.1, f32[2048]{0:T(1024)S(1)} %copy-done.4, ...), kind=kOutput, calls=%fused_computation.27 | convolution fusion | flops 5915148288 | bytes 18622464 | tf_op jit(solution)/shard_map/dot_general | solution.py:27
  497.4 0.0 reduce-scatter.2.cloned.1.call-update
  497.4 29.5 %reduce-scatter.2.cloned.1.call-done = bf16[512,512]{1,0:T(8,128)(2,1)} async-done(((bf16[512,2048]{1,0:T(8,128)(2,1)}), bf16[512,512]{1,0:T(8,128)(2,1)}) %reduce-scatter.2.cloned.1.call-update) | async-done | bytes 524304 | tf_op jit(solution)/shard_map/reduce_scatter | solution.py:99
  526.9 2.0 add_convert_fusion
  (14 shorter events, 0.0 us)
Async XLA Ops:
  6.5 74.4 %copy-start.3 = (f32[2048]{0:T(1024)S(1)}, f32[2048]{0:T(1024)}, u32[]{:S(2)}) copy-start(f32[2048]{0:T(1024)} %param.11) | copy-start | bytes 24580
  6.5 72.1 %all-gather.9.cloned.1.call-start = ((), (), s32[]{:S(2)}) async-start(), calls=%async_computation.1 | async-start | bytes 2621440 | tf_op jit(solution)/shard_map/all_gather | solution.py:61
  7.3 87.8 %all-gather.11.cloned.1.call-start = ((), (), s32[]{:S(2)}) async-start(), calls=%async_computation.2 | async-start | bytes 2359296 | tf_op jit(solution)/shard_map/all_gather | solution.py:63
  8.0 134.8 %all-gather.13.cloned.1.call-start = ((), (), s32[]{:S(2)}) async-start(), calls=%async_computation.3 | async-start | bytes 2359296 | tf_op jit(solution)/shard_map/all_gather | solution.py:83
  8.7 195.0 %all-gather.21.cloned.1.call-start = ((), (), s32[]{:S(2)}) async-start(), calls=%async_computation.8 | async-start | bytes 10485760 | tf_op jit(solution)/shard_map/all_gather | solution.py:11
  78.6 10.2 %copy-start = (bf16[512,2048]{1,0:T(8,128)(2,1)S(1)}, bf16[512,2048]{1,0:T(8,128)(2,1)}, u32[]{:S(2)}) copy-start(bf16[512,2048]{1,0:T(8,128)(2,1)} %all-gather.9.cloned.1.call-done) | copy-start | bytes 6291460
  78.6 10.2 %copy-start.2 = (bf16[2048,128]{1,0:T(8,128)(2,1)S(1)}, bf16[2048,128]{1,0:T(8,128)(2,1)}, u32[]{:S(2)}) copy-start(bf16[2048,128]{1,0:T(8,128)(2,1)} %all_gather.31) | copy-start | bytes 1572868
  83.3 14.8 %collective-permute-start.2 = (bf16[512,128]{1,0:T(8,128)(2,1)S(1)}, bf16[512,128]{1,0:T(8,128)(2,1)S(1)}, u32[]{:S(2)}, u32[]{:S(2)}) collective-permute-start(bf16[512,128]{1,0:T(8,128)(2,1)S(1)} %convolution_convert_fusion.3), channel_id=1, source_target_pairs={{0,8},{4,12},{8,16},{12,20},{16,24},{20,28},{1,9},{5,13},{9,17},{1... | collective-permute-start | bytes 393224 | tf_op jit(solution)/shard_map/ppermute | solution.py:17
  84.6 13.5 %collective-permute-start.3 = (bf16[512,128]{1,0:T(8,128)(2,1)S(1)}, bf16[512,128]{1,0:T(8,128)(2,1)}, u32[]{:S(2)}, u32[]{:S(2)}) collective-permute-start(bf16[512,128]{1,0:T(8,128)(2,1)S(1)} %convolution_convert_fusion.3), channel_id=1, source_target_pairs={{0,4},{4,8},{8,12},{12,16},{16,20},{20,24},{24,28},{1,5},{5,9},{9,... | collective-permute-start | bytes 393224 | tf_op jit(solution)/shard_map/ppermute | solution.py:17
  89.6 14.5 %collective-permute-start = (bf16[512,128]{1,0:T(8,128)(2,1)S(1)}, bf16[512,128]{1,0:T(8,128)(2,1)S(1)}, u32[]{:S(2)}, u32[]{:S(2)}) collective-permute-start(bf16[512,128]{1,0:T(8,128)(2,1)S(1)} %convolution_convert_fusion.4), channel_id=1, source_target_pairs={{0,8},{4,12},{8,16},{12,20},{16,24},{20,28},{1,9},{5,13},{9,17},{1... | collective-permute-start | bytes 393224 | tf_op jit(solution)/shard_map/ppermute | solution.py:17
  92.4 11.8 %collective-permute-start.1 = (bf16[512,128]{1,0:T(8,128)(2,1)S(1)}, bf16[512,128]{1,0:T(8,128)(2,1)S(1)}, u32[]{:S(2)}, u32[]{:S(2)}) collective-permute-start(bf16[512,128]{1,0:T(8,128)(2,1)S(1)} %convolution_convert_fusion.4), channel_id=1, source_target_pairs={{0,4},{4,8},{8,12},{12,16},{16,20},{20,24},{24,28},{1,5},{5,9},{9,... | collective-permute-start | bytes 393224 | tf_op jit(solution)/shard_map/ppermute | solution.py:17
  147.2 151.0 %all-gather.15.cloned.1.call-start = ((), (), s32[]{:S(2)}) async-start(), calls=%async_computation.4 | async-start | bytes 6488064 | tf_op jit(solution)/shard_map/all_gather | solution.py:92
  147.7 242.9 %all-gather.17.cloned.1.call-start = ((), (), s32[]{:S(2)}) async-start(), calls=%async_computation.5 | async-start | bytes 6488064 | tf_op jit(solution)/shard_map/all_gather | solution.py:93
  148.3 335.8 %all-gather.19.cloned.1.call-start = ((), (), s32[]{:S(2)}) async-start(), calls=%async_computation.6 | async-start | bytes 6488064 | tf_op jit(solution)/shard_map/all_gather | solution.py:97
  149.1 377.8 %reduce-scatter.2.cloned.1.call-start = ((), (), s32[]{:S(2)}) async-start(), calls=%async_computation.7 | async-start | bytes 2621440 | tf_op jit(solution)/shard_map/reduce_scatter | solution.py:99
  211.0 87.2 %copy-start.4 = (f32[2048]{0:T(1024)S(1)}, f32[2048]{0:T(1024)}, u32[]{:S(2)}) copy-start(f32[2048]{0:T(1024)} %param.16) | copy-start | bytes 24580
  298.1 185.9 %copy-start.1 = (bf16[512,2048]{1,0:T(8,128)(2,1)S(1)}, bf16[512,2048]{1,0:T(8,128)(2,1)}, u32[]{:S(2)}) copy-start(bf16[512,2048]{1,0:T(8,128)(2,1)} %get-tuple-element.6) | copy-start | bytes 6291460
Sparse Core Ops, SparseCore 0:
  8.9 25.2 all-gather.8
  36.3 52.5 all-gather.10
  91.0 51.7 all-gather.12
  147.3 56.4 all-gather.20
  205.8 92.2 all-gather.14
  300.2 90.4 all-gather.16
  392.7 91.2 all-gather.18
  497.5 29.3 reduce-scatter.1
